TPU v7x, 32 devices: a whole 2x2x4 slice. The times are simulated.
32 devices in a mesh: row: 8 (over z, y), col: 4 (over x, core).
Axes of the slice: x: 2, y: 2, z: 4, core: 2. Of those that a mesh axis runs over, the one named last changes fastest.
Arguments:
- layer_input: bfloat16 [2048, 8192], P('row'), may hold values from -7 to 7
- gain: float32 [8192], replicated, may hold values from 0.5 to 6
- d_query: bfloat16 [2048, 4096], P('row', 'col'), may hold values from -6 to 6
- d_keyval: bfloat16 [2048, 2048], P('row', 'col'), may hold values from -6 to 6
- w_query: bfloat16 [8192, 4096], P('row', 'col'), may hold values from -0.0625 to 0.0625
- w_keyval: bfloat16 [8192, 2048], P('row', 'col'), may hold values from -1 to 1
- d_resid: bfloat16 [2048, 8192], P('row', 'col'), may hold values from -6 to 6
Outputs:
- d_input: bfloat16 [2048, 8192], P('row', 'col')
- grad_wq: bfloat16 [8192, 4096], P('row', 'col')
- grad_wkv: bfloat16 [8192, 2048], P('row', 'col')
- grad_gain: float32 [8192], P('col')
- grad_square_sum: float32 [], replicated
All inputs are finite; a program needn't handle non-finite values.
Results may differ from a plain program's by a relative error of at most 0.023.
Values may be sent and summed in bfloat16 or wider, within the bound.
A program may use at most 128 MiB of HBM per device.

v0:
```python
import math

import jax
import jax.numpy as jnp
from jax import lax
from jax.sharding import PartitionSpec as P

epsilon = 1e-05


def local(layer_input, gain, d_query, d_keyval, w_query, w_keyval, d_resid):
    inputs = layer_input.astype(jnp.float32)
    inv_rms = lax.rsqrt(jnp.mean(inputs * inputs, axis=1, keepdims=True) + epsilon)
    normed = (inputs * inv_rms * gain).astype(jnp.bfloat16)
    model_width = inputs.shape[1]
    local_tokens = inputs.shape[0]
    tokens_all = local_tokens * lax.axis_size("row")
    scaling = 1.0 / math.sqrt(tokens_all)
    weight_scale = 1.0 / math.sqrt(local_tokens)
    contract_cols = (((1,), (1,)), ((), ()))
    partial_value = lax.dot_general(
        d_query,
        lax.all_gather(w_query, "row", axis=0, tiled=True),
        contract_cols,
        preferred_element_type=jnp.float32,
    )
    partial_value = partial_value + lax.dot_general(
        d_keyval,
        lax.all_gather(w_keyval, "row", axis=0, tiled=True),
        contract_cols,
        preferred_element_type=jnp.float32,
    )
    rounded = lax.optimization_barrier(partial_value.astype(jnp.bfloat16)).astype(jnp.float32)
    feature_grad = lax.psum_scatter(
        rounded.astype(jnp.bfloat16), "col", scatter_dimension=1, tiled=True
    ).astype(jnp.float32)
    slice_width = feature_grad.shape[1]
    col_start = lax.axis_index("col") * slice_width
    input_part = lax.dynamic_slice_in_dim(inputs, col_start, slice_width, 1)
    gain_part = lax.dynamic_slice_in_dim(gain, col_start, slice_width, 0)
    weighted = gain_part * feature_grad
    token_dot = lax.psum(jnp.sum(weighted * input_part, axis=1, keepdims=True), "col")
    d_input = (
        d_resid.astype(jnp.float32)
        + inv_rms * weighted
        - input_part * inv_rms**3 * token_dot / model_width
    ).astype(jnp.bfloat16)
    gain_partial = jnp.sum(feature_grad * input_part * inv_rms, axis=0) * scaling
    cotangent = jnp.concatenate([d_query, d_keyval], axis=1)
    query_cols = d_query.shape[1]
    columns = lax.all_to_all(normed, "row", split_axis=1, concat_axis=0, tiled=True)
    all_cotangents = lax.all_gather(cotangent, "row", axis=0, tiled=True)
    groups = lax.axis_size("row")
    column_blocks = columns.reshape(groups, local_tokens, columns.shape[1])
    grad_blocks = all_cotangents.reshape(groups, local_tokens, all_cotangents.shape[1])
    blocks = (
        lax.dot_general(
            column_blocks,
            grad_blocks,
            (((1,), (1,)), ((0,), (0,))),
            preferred_element_type=jnp.float32,
        )
        * weight_scale
    )
    summed = jnp.sum(blocks.astype(jnp.bfloat16).astype(jnp.float32), axis=0)
    grad_wq = summed[:, :query_cols].astype(jnp.bfloat16)
    grad_wkv = summed[:, query_cols:].astype(jnp.bfloat16)
    query_f = grad_wq.astype(jnp.float32)
    keyval_f = grad_wkv.astype(jnp.float32)
    tile_square = jnp.sum(query_f * query_f) + jnp.sum(keyval_f * keyval_f)
    grad_gain = lax.psum(gain_partial, "row")
    leading = jnp.where(
        lax.axis_index("row") == 0, jnp.sum(grad_gain * grad_gain), jnp.float32(0.0)
    )
    grand_total = lax.psum(tile_square + leading, ("row", "col"))
    grad_square_sum = grand_total / jnp.float32(model_width)
    return (d_input, grad_wq, grad_wkv, grad_gain, grad_square_sum)


def solution(mesh):
    placed = (
        P("row", None),
        P(),
        P("row", "col"),
        P("row", "col"),
        P("row", "col"),
        P("row", "col"),
        P("row", "col"),
    )
    return jax.shard_map(
        local,
        mesh=mesh,
        in_specs=placed,
        out_specs=(P("row", "col"), P("row", "col"), P("row", "col"), P("col"), P()),
        check_vma=False,
    )
```

profile of v0, /device:TPU:12, one launch (start us, length us, event | category | flops | bytes accessed | tf_op | source)
XLA Modules:
  0.0 671.1 jit_solution(14180824158022452798)
XLA Ops:
  7.2 0.0 all-gather.6.cloned.1.call-start
  7.2 0.7 all-gather.6.cloned.1.call-update
  7.9 0.0 copy-start.4
  7.9 0.0 all-gather.4.cloned.1.call-start
  8.0 0.7 all-gather.4.cloned.1.call-update
  8.7 0.0 all-gather.8.cloned.1.call-start
  8.7 2.1 pad_maximum_fusion
  10.8 0.0 all-gather.8.cloned.1.call-update
  10.8 0.0 copy-start
  10.8 3.3 multiply_reduce_fusion
  14.1 0.0 copy-done.4
  14.1 0.2 copy-done
  14.2 3.2 multiply_convert_fusion.1
  17.4 6.5 copy.13
  23.9 0.0 copy-start.2
  23.9 6.4 all-to-all-start
  30.3 0.0 copy-start.1
  30.3 0.0 reduce-scatter.2.cloned.1.call-start
  30.3 181.7 %all-gather.6.cloned.1.call-done = bf16[8192,512]{1,0:T(8,128)(2,1)} async-done(((bf16[1024,512]{1,0:T(8,128)(2,1)}), bf16[8192,512]{1,0:T(8,128)(2,1)}) %all-gather.6.cloned.1.call-update) | async-done | bytes 8388624 | tf_op jit(solution)/shard_map/all_gather | solution.py:29
  212.0 0.0 copy-done.2
  212.1 9.0 %fusion.11 = f32[256,8192]{1,0:T(8,128)} fusion(bf16[256,512]{1,0:T(8,128)(2,1)S(1)} %copy-done.2, bf16[8192,512]{1,0:T(8,128)(2,1)} %all-gather.6.cloned.1.call-done), kind=kOutput, calls=%fused_computation.24 | convolution fusion | flops 2147483648 | bytes 17039360 | tf_op jit(solution)/shard_map/dot_general | solution.py:27
  221.0 219.9 %all-gather.4.cloned.1.call-done = bf16[8192,1024]{1,0:T(8,128)(2,1)} async-done(((bf16[1024,1024]{1,0:T(8,128)(2,1)}), bf16[8192,1024]{1,0:T(8,128)(2,1)}) %all-gather.4.cloned.1.call-update) | async-done | bytes 16777232 | tf_op jit(solution)/shard_map/all_gather | solution.py:23
  440.9 0.0 copy-done.1
  440.9 12.4 %fusion = bf16[256,8192]{1,0:T(8,128)(2,1)} fusion(f32[256,8192]{1,0:T(8,128)} %fusion.11, bf16[256,1024]{1,0:T(8,128)(2,1)S(1)} %copy-done.1, bf16[8192,1024]{1,0:T(8,128)(2,1)} %all-gather.4.cloned.1.call-done), kind=kOutput, calls=%fused_computation.2 | convolution fusion | flops 4299161600 | bytes 29884416 | tf_op jit(solution)/shard_map/dot_general | solution.py:21
  453.4 0.0 reduce-scatter.2.cloned.1.call-update
  453.4 6.7 convert_element_type.35
  460.0 0.0 all-to-all-done
  460.0 81.3 %all-gather.8.cloned.1.call-done = bf16[2048,1536]{1,0:T(8,128)(2,1)} async-done(((bf16[256,1536]{1,0:T(8,128)(2,1)}), bf16[2048,1536]{1,0:T(8,128)(2,1)}) %all-gather.8.cloned.1.call-update) | async-done | bytes 6291472 | tf_op jit(solution)/shard_map/all_gather | solution.py:52
  541.3 10.9 %fusion.1 = bf16[1024,1536]{1,0:T(8,128)(2,1)S(1)} fusion(bf16[8,256,1536]{2,1,0:T(8,128)(2,1)} %bitcast.11, bf16[256,8,1024]{0,2,1:T(8,128)(2,1)} %all-to-all-done), kind=kOutput, calls=%fused_computation.5 | convolution fusion | flops 6478626816 | bytes 13631488 | tf_op jit(solution)/shard_map/dot_general | solution.py:57
  552.2 2.0 multiply_reduce_fusion.2
  554.3 0.0 copy-start.3
  554.3 2.9 multiply_reduce_fusion.1
  558.5 29.9 %reduce-scatter.2.cloned.1.call-done = bf16[256,2048]{1,0:T(8,128)(2,1)} async-done(((bf16[256,8192]{1,0:T(8,128)(2,1)}), bf16[256,2048]{1,0:T(8,128)(2,1)}) %reduce-scatter.2.cloned.1.call-update) | async-done | bytes 1048592 | tf_op jit(solution)/shard_map/reduce_scatter | solution.py:34
  588.4 2.6 fusion.10
  591.0 15.3 %psum.22 = f32[2048]{0:T(1024)S(1)} all-reduce(f32[2048]{0:T(1024)S(1)} %broadcast_multiply_fusion), channel_id=1, replica_groups=mesh['row'=8,'col'=4] {'row'}, use_global_device_ids=true, to_apply=%region_6.0 | all-reduce | flops 2048 | bytes 16384 | tf_op jit(solution)/shard_map/psum | solution.py:71
  606.3 0.0 copy-start.5
  606.3 0.6 multiply_reduce_fusion.3
  607.5 6.0 psum.21
  613.5 45.6 %psum.23 = f32[]{:T(128)} all-reduce(f32[]{:T(128)S(6)} %add.44), channel_id=1, replica_groups=mesh['row'=8,'col'=4] {'row','col'}, use_global_device_ids=true, to_apply=%region_10.11 | all-reduce | flops 1 | bytes 8 | tf_op jit(solution)/shard_map/psum | solution.py:75
  659.7 0.0 copy-done.3
  659.8 3.6 fusion.7
  663.4 0.0 copy-done.5
  (3 shorter events, 0.0 us)
Async XLA Ops:
  7.2 204.9 %all-gather.6.cloned.1.call-start = ((), (), s32[]{:S(2)}) async-start(), calls=%async_computation.3 | async-start | bytes 9437184 | tf_op jit(solution)/shard_map/all_gather | solution.py:29
  7.9 6.2 copy-start.4
  7.9 433.0 %all-gather.4.cloned.1.call-start = ((), (), s32[]{:S(2)}) async-start(), calls=%async_computation.2 | async-start | bytes 18874368 | tf_op jit(solution)/shard_map/all_gather | solution.py:23
  8.7 532.6 %all-gather.8.cloned.1.call-start = ((), (), s32[]{:S(2)}) async-start(), calls=%async_computation.5 | async-start | bytes 7077888 | tf_op jit(solution)/shard_map/all_gather | solution.py:52
  10.8 3.5 copy-start
  23.9 188.1 %copy-start.2 = (bf16[256,512]{1,0:T(8,128)(2,1)S(1)}, bf16[256,512]{1,0:T(8,128)(2,1)}, u32[]{:S(2)}) copy-start(bf16[256,512]{1,0:T(8,128)(2,1)} %param.10) | copy-start | bytes 786436
  23.9 436.1 %all-to-all-start = ((bf16[256,8,1024]{0,2,1:T(8,128)(2,1)}), bf16[256,8,1024]{0,2,1:T(8,128)(2,1)}, u32[]{:S(2)}, u32[]{:S(2)}) async-start(bf16[256,8,1024]{0,2,1:T(8,128)(2,1)} %bitcast.10), calls=%async_computation.1 | async-start | bytes 8388608 | tf_op jit(solution)/shard_map/all_to_all | solution.py:51
  30.3 410.6 %copy-start.1 = (bf16[256,1024]{1,0:T(8,128)(2,1)S(1)}, bf16[256,1024]{1,0:T(8,128)(2,1)}, u32[]{:S(2)}) copy-start(bf16[256,1024]{1,0:T(8,128)(2,1)} %param.9) | copy-start | bytes 1572868
  30.3 558.1 %reduce-scatter.2.cloned.1.call-start = ((), (), s32[]{:S(2)}) async-start(), calls=%async_computation.4 | async-start | bytes 5242880 | tf_op jit(solution)/shard_map/reduce_scatter | solution.py:34
  554.3 105.5 %copy-start.3 = (bf16[256,2048]{1,0:T(8,128)(2,1)S(1)}, bf16[256,2048]{1,0:T(8,128)(2,1)}, u32[]{:S(2)}) copy-start(bf16[256,2048]{1,0:T(8,128)(2,1)} %param.13) | copy-start | bytes 3145732
  606.3 57.1 %copy-start.5 = (f32[2048]{0:T(1024)}, f32[2048]{0:T(1024)S(1)}, u32[]{:S(2)}) copy-start(f32[2048]{0:T(1024)S(1)} %psum.22) | copy-start | bytes 24580
Sparse Core Ops, SparseCore 0:
  10.1 201.9 all-gather.5
  214.2 226.7 all-gather.3
  443.7 97.5 all-gather.7
  543.7 44.6 reduce-scatter.1
where the time goes:
time: 672 us; the launch traced here: 671 us
  waiting for transfers between devices  514 us (76%)
  blocking collectives  66.8 us (10%)
  matrix products  32.3 us (5%)
  other arithmetic  27 us (4%)
  between operations  17.6 us (3%)
    all_gather x1, waiting for transfers between devices, local(): lax.all_gather(w_query, 'row', axis=0, tiled=True)  220 us
    all_gather x1, waiting for transfers between devices, local(): lax.all_gather(w_keyval, 'row', axis=0, tiled=True)  182 us
    all_gather x1, waiting for transfers between devices, local(): all_cotangents = lax.all_gather(cotangent, 'row', axis=0, tiled=True)  81.3 us
    psum x1, blocking collectives, local(): grand_total = lax.psum(tile_square + leading, ('row', 'col'))  45.6 us
    reduce_scatter x1, waiting for transfers between devices, local(): lax.psum_scatter(rounded.astype(jnp.bfloat16), 'col', scatter_dimension=1...  29.9 us
    psum x1, blocking collectives, local(): grad_gain = lax.psum(gain_partial, 'row')  15.3 us
  transfers between devices with their start and end apart: 5, of which 4 were waited for; matrix products, arithmetic and copies ran while one was open for 9% of the time, Pallas kernels for 0%

commit v1 on v0

--- a/solution.py
+++ b/solution.py
@@ -18,21 +18,36 @@
     scaling = 1.0 / math.sqrt(tokens_all)
     weight_scale = 1.0 / math.sqrt(local_tokens)
     contract_cols = (((1,), (1,)), ((), ()))
+    query_cols = d_query.shape[1]
+    cotangent = jnp.concatenate([d_query, d_keyval], axis=1)
+    all_cotangents = lax.all_gather(cotangent, "row", axis=0, tiled=True)
+    weights = jnp.concatenate([w_query, w_keyval], axis=1)
     partial_value = lax.dot_general(
-        d_query,
-        lax.all_gather(w_query, "row", axis=0, tiled=True),
-        contract_cols,
-        preferred_element_type=jnp.float32,
+        all_cotangents, weights, contract_cols, preferred_element_type=jnp.float32
     )
-    partial_value = partial_value + lax.dot_general(
-        d_keyval,
-        lax.all_gather(w_keyval, "row", axis=0, tiled=True),
-        contract_cols,
-        preferred_element_type=jnp.float32,
+    reduced = lax.psum_scatter(
+        partial_value.astype(jnp.bfloat16), "col", scatter_dimension=0, tiled=True
     )
-    rounded = lax.optimization_barrier(partial_value.astype(jnp.bfloat16)).astype(jnp.float32)
-    feature_grad = lax.psum_scatter(
-        rounded.astype(jnp.bfloat16), "col", scatter_dimension=1, tiled=True
+    n_row, n_col = lax.axis_size("row"), lax.axis_size("col")
+    fold = n_row // n_col
+    pieces = reduced.reshape(fold, local_tokens, reduced.shape[1])
+    row, col = lax.axis_index("row"), lax.axis_index("col")
+    arrived = []
+    for shift in range(fold):
+        pairs = [
+            (r * n_col + c, (fold * c + (r + shift) % fold) * n_col + r // fold)
+            for r in range(n_row)
+            for c in range(n_col)
+        ]
+        piece = lax.dynamic_index_in_dim(pieces, (row + shift) % fold, 0, keepdims=False)
+        arrived.append(lax.ppermute(piece, ("row", "col"), pairs))
+    arrived = jnp.stack(arrived)
+    feature_grad = jnp.concatenate(
+        [
+            lax.dynamic_index_in_dim(arrived, (row - j + fold) % fold, 0, keepdims=False)
+            for j in range(fold)
+        ],
+        axis=1,
     ).astype(jnp.float32)
     slice_width = feature_grad.shape[1]
     col_start = lax.axis_index("col") * slice_width
@@ -47,9 +62,7 @@
     ).astype(jnp.bfloat16)
     gain_partial = jnp.sum(feature_grad * input_part * inv_rms, axis=0) * scaling
     cotangent = jnp.concatenate([d_query, d_keyval], axis=1)
-    query_cols = d_query.shape[1]
     columns = lax.all_to_all(normed, "row", split_axis=1, concat_axis=0, tiled=True)
-    all_cotangents = lax.all_gather(cotangent, "row", axis=0, tiled=True)
     groups = lax.axis_size("row")
     column_blocks = columns.reshape(groups, local_tokens, columns.shape[1])
     grad_blocks = all_cotangents.reshape(groups, local_tokens, all_cotangents.shape[1])

time: 672 us -> 377 us (0.56)
  waiting for transfers between devices: 514 us -> 198 us
  blocking collectives: 66.8 us -> 91.9 us
  matrix products: 32.3 us -> 21.3 us
    all_gather x2 -> x0, waiting for transfers between devices: 402 us -> none  [the longest x1 220 us: local(): lax.all_gather(w_query, 'row', axis=0, tiled=True)]
    all_gather x1, waiting for transfers between devices: 81.3 us -> 150 us  [local(): all_cotangents = lax.all_gather(cotangent, 'row', axis=0, tiled=True)]
    psum x1, blocking collectives: 15.3 us -> 39.8 us  [local(): grad_gain = lax.psum(gain_partial, 'row')]
    ppermute x0 -> x2, waiting for transfers between devices: none -> 11.7 us  [local(): arrived.append(lax.ppermute(piece, ('row', 'col'), pairs))]
    dot_general x2 -> x1, matrix products: 21.4 us -> 10.4 us  [local(): lax.dot_general(all_cotangents, weights, contract_cols, preferred_element...]
  transfers between devices with their start and end apart: 5 -> 5, of which waited for: 4 -> 4; matrix products, arithmetic and copies ran while one was open for 9% -> 12% of each run, Pallas kernels for 0% -> 0%
where the time goes in v1:
time: 377 us; the launch traced here: 376 us
  waiting for transfers between devices  198 us (53%)
  blocking collectives  91.9 us (24%)
  other arithmetic  27.5 us (7%)
  matrix products  21.3 us (6%)
  between operations  18 us (5%)
  starting transfers between devices  10.2 us (3%)
  local copies, waits for them, and re-layouts  8.93 us (2%)
    all_gather x1, waiting for transfers between devices, local(): all_cotangents = lax.all_gather(cotangent, 'row', axis=0, tiled=True)  150 us
    psum x1, blocking collectives, local(): grand_total = lax.psum(tile_square + leading, ('row', 'col'))  46.5 us
    psum x1, blocking collectives, local(): grad_gain = lax.psum(gain_partial, 'row')  39.8 us
    reduce_scatter x1, waiting for transfers between devices, local(): lax.psum_scatter(partial_value.astype(jnp.bfloat16), 'col', scatter_dimen...  36.4 us
    ppermute x2, waiting for transfers between devices, local(): arrived.append(lax.ppermute(piece, ('row', 'col'), pairs))  11.7 us
    dot_general x1, matrix products, local(): lax.dot_general(column_blocks, grad_blocks, (((1,), (1,)), ((0,), (0,))),...  10.9 us
    dot_general x1, matrix products, local(): lax.dot_general(all_cotangents, weights, contract_cols, preferred_element...  10.4 us
  transfers between devices with their start and end apart: 5, of which 4 were waited for; matrix products, arithmetic and copies ran while one was open for 12% of the time, Pallas kernels for 0%

profile of v1, /device:TPU:12, one launch (start us, length us, event | category | flops | bytes accessed | tf_op | source)
XLA Modules:
  0.0 376.0 jit_solution(1316032979656445743)
XLA Ops:
  7.2 0.0 copy-start.2
  7.2 0.0 all-gather.2.cloned.1.call-start
  7.2 2.1 pad_maximum_fusion.1
  9.3 0.0 all-gather.2.cloned.1.call-update
  9.3 0.0 copy-start
  9.3 3.3 multiply_reduce_fusion
  12.6 0.0 copy-done.2
  12.6 0.2 copy-done
  12.8 3.1 multiply_convert_fusion.1
  15.9 6.5 %copy.12 = bf16[256,8192]{0,1:T(8,128)(2,1)} copy(bf16[256,8192]{1,0:T(8,128)(2,1)} %multiply_convert_fusion.1) | data formatting | bytes 8388608 | tf_op jit(solution)/shard_map/convert_element_type | solution.py:14
  22.3 0.0 copy-start.4
  22.3 6.3 %all-to-all-start = ((bf16[256,8,1024]{0,2,1:T(8,128)(2,1)}), bf16[256,8,1024]{0,2,1:T(8,128)(2,1)}, u32[]{:S(2)}, u32[]{:S(2)}) async-start(bf16[256,8,1024]{0,2,1:T(8,128)(2,1)} %bitcast.18), calls=%async_computation.1 | async-start | bytes 8388608 | tf_op jit(solution)/shard_map/all_to_all | solution.py:65
  28.7 0.0 reduce-scatter.2.cloned.1.call-start
  28.7 150.1 %all-gather.2.cloned.1.call-done = bf16[2048,1536]{1,0:T(8,128)(2,1)} async-done(((bf16[256,1536]{1,0:T(8,128)(2,1)}), bf16[2048,1536]{1,0:T(8,128)(2,1)}) %all-gather.2.cloned.1.call-update) | async-done | bytes 6291472 | tf_op jit(solution)/shard_map/all_gather | solution.py:23
  178.7 0.0 copy-done.4
  178.8 10.4 %convolution_convert_fusion = bf16[2048,1024]{1,0:T(8,128)(2,1)} fusion(bf16[2048,1536]{1,0:T(8,128)(2,1)} %all-gather.2.cloned.1.call-done, bf16[1024,512]{1,0:T(8,128)(2,1)} %param.12, bf16[1024,1024]{1,0:T(8,128)(2,1)S(1)} %copy-done.4), kind=kOutput, calls=%fused_computation.6 | convolution fusion | flops 6450839552 | bytes 13631488 | tf_op jit(solution)/shard_map/dot_general | solution.py:25
  189.2 0.0 reduce-scatter.2.cloned.1.call-update
  189.2 6.4 %convert_element_type.33 = f32[256,8192]{1,0:T(8,128)} convert(bf16[256,8192]{1,0:T(8,128)(2,1)} %param.7) | non-fusion elementwise | flops 2097152 | bytes 12582912 | tf_op jit(solution)/shard_map/convert_element_type | solution.py:12
  195.6 0.0 all-to-all-done
  195.6 10.9 %fusion = bf16[1024,1536]{1,0:T(8,128)(2,1)S(1)} fusion(bf16[8,256,1536]{2,1,0:T(8,128)(2,1)} %bitcast.20, bf16[256,8,1024]{0,2,1:T(8,128)(2,1)} %all-to-all-done), kind=kOutput, calls=%fused_computation.3 | convolution fusion | flops 6478626816 | bytes 13631488 | tf_op jit(solution)/shard_map/dot_general | solution.py:70
  206.6 36.4 %reduce-scatter.2.cloned.1.call-done = bf16[512,1024]{1,0:T(8,128)(2,1)} async-done(((bf16[2048,1024]{1,0:T(8,128)(2,1)}), bf16[512,1024]{1,0:T(8,128)(2,1)}) %reduce-scatter.2.cloned.1.call-update) | async-done | bytes 1048592 | tf_op jit(solution)/shard_map/reduce_scatter | solution.py:28
  243.0 2.3 dynamic-slice_bitcast_fusion
  245.2 0.0 collective-permute-start.1
  245.2 3.8 %collective-permute-start = (bf16[256,1024]{1,0:T(8,128)(2,1)}, bf16[256,1024]{1,0:T(8,128)(2,1)}, u32[]{:S(2)}, u32[]{:S(2)}) collective-permute-start(bf16[256,1024]{1,0:T(8,128)(2,1)} %get-tuple-element.14), channel_id=1, source_target_pairs={{0,0},{1,8},{2,16},{3,24},{4,4},{5,12},{6,20},{7,28},{8,1},{9,9},{... | collective-permute-start | bytes 1572872 | tf_op jit(solution)/shard_map/ppermute | solution.py:43
  249.1 2.0 multiply_reduce_fusion.2
  251.1 2.9 multiply_reduce_fusion.1
  254.0 0.0 copy-start.1
  255.4 0.4 collective-permute-done.1
  255.9 11.2 %collective-permute-done = bf16[256,1024]{1,0:T(8,128)(2,1)} collective-permute-done((bf16[256,1024]{1,0:T(8,128)(2,1)}, bf16[256,1024]{1,0:T(8,128)(2,1)}, u32[]{:S(2)}, u32[]{:S(2)}) %collective-permute-start) | collective-permute-done | bytes 524320 | tf_op jit(solution)/shard_map/ppermute | solution.py:43
  267.1 1.6 fusion.16
  268.7 2.2 fusion.12
  270.9 39.8 %psum.22 = f32[2048]{0:T(1024)S(1)} all-reduce(f32[2048]{0:T(1024)S(1)} %broadcast_multiply_fusion), channel_id=1, replica_groups=mesh['row'=8,'col'=4] {'row'}, use_global_device_ids=true, to_apply=%region_6.7 | all-reduce | flops 2048 | bytes 16384 | tf_op jit(solution)/shard_map/psum | solution.py:84
  310.7 0.0 copy-start.3
  310.7 0.6 multiply_reduce_fusion.3
  312.0 46.5 %psum.23 = f32[]{:T(128)} all-reduce(f32[]{:T(128)S(6)} %add.80), channel_id=1, replica_groups=mesh['row'=8,'col'=4] {'row','col'}, use_global_device_ids=true, to_apply=%region_10.11 | all-reduce | flops 1 | bytes 8 | tf_op jit(solution)/shard_map/psum | solution.py:88
  358.5 5.6 %psum.21 = f32[256]{0:T(256)S(1)} all-reduce(f32[256]{0:T(256)S(1)} %get-tuple-element.6), channel_id=1, replica_groups=mesh['row'=8,'col'=4] {'col'}, use_global_device_ids=true, to_apply=%region_3.4 | all-reduce | flops 256 | bytes 2048 | tf_op jit(solution)/shard_map/psum | solution.py:57
  364.7 0.0 copy-done.1
  364.7 3.3 fusion.9
  368.0 0.0 copy-done.3
  (3 shorter events, 0.0 us)
Async XLA Ops:
  7.2 5.4 %copy-start.2 = (f32[8192]{0:T(1024)S(1)}, f32[8192]{0:T(1024)}, u32[]{:S(2)}) copy-start(f32[8192]{0:T(1024)} %param.8) | copy-start | bytes 98308
  7.2 171.6 %all-gather.2.cloned.1.call-start = ((), (), s32[]{:S(2)}) async-start(), calls=%async_computation.2 | async-start | bytes 7077888 | tf_op jit(solution)/shard_map/all_gather | solution.py:23
  9.3 3.5 copy-start
  22.3 156.4 %copy-start.4 = (bf16[1024,1024]{1,0:T(8,128)(2,1)S(1)}, bf16[1024,1024]{1,0:T(8,128)(2,1)}, u32[]{:S(2)}) copy-start(bf16[1024,1024]{1,0:T(8,128)(2,1)} %param.11) | copy-start | bytes 6291460
  22.3 173.3 %all-to-all-start = ((bf16[256,8,1024]{0,2,1:T(8,128)(2,1)}), bf16[256,8,1024]{0,2,1:T(8,128)(2,1)}, u32[]{:S(2)}, u32[]{:S(2)}) async-start(bf16[256,8,1024]{0,2,1:T(8,128)(2,1)} %bitcast.18), calls=%async_computation.1 | async-start | bytes 8388608 | tf_op jit(solution)/shard_map/all_to_all | solution.py:65
  28.7 214.3 %reduce-scatter.2.cloned.1.call-start = ((), (), s32[]{:S(2)}) async-start(), calls=%async_computation.3 | async-start | bytes 5242880 | tf_op jit(solution)/shard_map/reduce_scatter | solution.py:28
  245.2 10.6 %collective-permute-start.1 = (bf16[256,1024]{1,0:T(8,128)(2,1)}, bf16[256,1024]{1,0:T(8,128)(2,1)}, u32[]{:S(2)}, u32[]{:S(2)}) collective-permute-start(bf16[256,1024]{1,0:T(8,128)(2,1)} %get-tuple-element.13), channel_id=1, source_target_pairs={{0,4},{1,12},{2,20},{3,28},{4,0},{5,8},{6,16},{7,24},{8,5},{9,13},... | collective-permute-start | bytes 1572872 | tf_op jit(solution)/shard_map/ppermute | solution.py:43
  245.2 21.9 %collective-permute-start = (bf16[256,1024]{1,0:T(8,128)(2,1)}, bf16[256,1024]{1,0:T(8,128)(2,1)}, u32[]{:S(2)}, u32[]{:S(2)}) collective-permute-start(bf16[256,1024]{1,0:T(8,128)(2,1)} %get-tuple-element.14), channel_id=1, source_target_pairs={{0,0},{1,8},{2,16},{3,24},{4,4},{5,12},{6,20},{7,28},{8,1},{9,9},{... | collective-permute-start | bytes 1572872 | tf_op jit(solution)/shard_map/ppermute | solution.py:43
  254.0 110.7 %copy-start.1 = (bf16[256,2048]{1,0:T(8,128)(2,1)S(1)}, bf16[256,2048]{1,0:T(8,128)(2,1)}, u32[]{:S(2)}) copy-start(bf16[256,2048]{1,0:T(8,128)(2,1)} %param.13) | copy-start | bytes 3145732
  310.7 57.3 %copy-start.3 = (f32[2048]{0:T(1024)}, f32[2048]{0:T(1024)S(1)}, u32[]{:S(2)}) copy-start(f32[2048]{0:T(1024)S(1)} %psum.22) | copy-start | bytes 24580
Sparse Core Ops, SparseCore 0:
  10.7 167.9 all-gather.1
  189.3 53.6 reduce-scatter.1

commit v2 on v1

--- a/solution.py
+++ b/solution.py
@@ -1,11 +1,216 @@
+import functools
 import math
 
 import jax
 import jax.numpy as jnp
 from jax import lax
+from jax.experimental import pallas as pl
+from jax.experimental.pallas import tpu as pltpu
 from jax.sharding import PartitionSpec as P
 
 epsilon = 1e-05
+MESH = pl.DeviceIdType.MESH
+PIECES = 2
+
+
+def ring_order(place, n):
+    return jnp.where(place < n // 2, 2 * place, 2 * (n - 1 - place) + 1)
+
+
+def ring_place(index, n):
+    half = index // 2
+    return jnp.where(index % 2 == 0, half, n - 1 - half)
+
+
+def greet(row, col, n_row, n_col):
+    barrier = pltpu.get_barrier_semaphore()
+    for k in range(1, n_row):
+        pl.semaphore_signal(
+            barrier, inc=1, device_id=((row + k) % n_row, col), device_id_type=MESH
+        )
+    for k in range(1, n_col):
+        pl.semaphore_signal(
+            barrier, inc=1, device_id=(row, (col + k) % n_col), device_id_type=MESH
+        )
+    pl.semaphore_wait(barrier, n_row + n_col - 2)
+
+
+def gather_kernel(
+    n_row, n_col, cot, normed, all_cot, columns,
+    own_sem, ring_send, ring_recv, swap_send, swap_recv, share_send, share_recv,
+):
+    row, col = lax.axis_index("row"), lax.axis_index("col")
+    tokens = cot.shape[0]
+    width = columns.shape[2]
+    part = tokens // n_col
+    piece = tokens // (2 * PIECES)
+    place = ring_place(row, n_row)
+    ahead = ring_order((place + 1) % n_row, n_row)
+    behind = ring_order((place + n_row - 1) % n_row, n_row)
+    greet(row, col, n_row, n_col)
+
+    own_rows = pl.ds(pl.multiple_of(col * part, part), part)
+
+    def ring_copy(step, way, q):
+        if way == 0:
+            source, target = ring_order((place + n_row - step) % n_row, n_row), ahead
+        else:
+            source, target = ring_order((place + step) % n_row, n_row), behind
+        rows = pl.ds((way * PIECES + q) * piece, piece)
+        return pltpu.make_async_remote_copy(
+            src_ref=cot.at[rows] if step == 0 else all_cot.at[source, rows],
+            dst_ref=all_cot.at[source, rows],
+            send_sem=ring_send.at[step, way, q],
+            recv_sem=ring_recv.at[step, way, q],
+            device_id=(target, col),
+            device_id_type=MESH,
+        )
+
+    def swap_copy(k):
+        target = ring_order((place + k) % n_row, n_row)
+        return pltpu.make_async_remote_copy(
+            src_ref=normed.at[own_rows, pl.ds(pl.multiple_of(target * width, width), width)],
+            dst_ref=columns.at[row, own_rows],
+            send_sem=swap_send.at[k],
+            recv_sem=swap_recv.at[k],
+            device_id=(target, col),
+            device_id_type=MESH,
+        )
+
+    own_columns = pl.ds(pl.multiple_of(row * width, width), width)
+
+    def share_copy(k, j):
+        source = ring_order((place + n_row - k) % n_row, n_row)
+        return pltpu.make_async_remote_copy(
+            src_ref=columns.at[source, own_rows],
+            dst_ref=columns.at[source, own_rows],
+            send_sem=share_send.at[k, j],
+            recv_sem=share_recv.at[k, j],
+            device_id=(row, (col + j) % n_col),
+            device_id_type=MESH,
+        )
+
+    keep_cot = pltpu.make_async_copy(cot, all_cot.at[row], own_sem.at[0])
+    keep_normed = pltpu.make_async_copy(
+        normed.at[:, own_columns], columns.at[row], own_sem.at[1]
+    )
+    rings = {}
+    swaps = {}
+    shares = []
+    for step in range(n_row):
+        for q in range(PIECES):
+            for way in range(2):
+                if step > 0:
+                    rings[step - 1, way, q].wait_recv()
+                if step < n_row - 1:
+                    rings[step, way, q] = ring_copy(step, way, q)
+                    rings[step, way, q].start()
+        if step == 0:
+            keep_cot.start()
+            keep_normed.start()
+        if step < n_row - 1:
+            swaps[step + 1] = swap_copy(step + 1)
+            swaps[step + 1].start()
+        if step > 0:
+            swaps[step].wait_recv()
+            for j in range(1, n_col):
+                copy = share_copy(step, j)
+                copy.start()
+                shares.append(copy)
+    keep_cot.wait()
+    keep_normed.wait()
+    for copy in list(rings.values()) + list(swaps.values()):
+        copy.wait_send()
+    for copy in shares:
+        copy.wait()
+
+
+def gather(cot, normed, n_row, n_col):
+    tokens, cot_width = cot.shape
+    width = normed.shape[1] // n_row
+    dma = pltpu.SemaphoreType.DMA
+    return pl.pallas_call(
+        functools.partial(gather_kernel, n_row, n_col),
+        out_shape=(
+            jax.ShapeDtypeStruct((n_row, tokens, cot_width), cot.dtype),
+            jax.ShapeDtypeStruct((n_row, tokens, width), normed.dtype),
+        ),
+        in_specs=[pl.BlockSpec(memory_space=pltpu.VMEM)] * 2,
+        out_specs=[pl.BlockSpec(memory_space=pl.ANY)] * 2,
+        scratch_shapes=[
+            dma((2,)),
+            dma((n_row, 2, PIECES)),
+            dma((n_row, 2, PIECES)),
+            dma((n_row,)),
+            dma((n_row,)),
+            dma((n_row, n_col)),
+            dma((n_row, n_col)),
+        ],
+        compiler_params=pltpu.CompilerParams(collective_id=0, has_side_effects=True),
+        name="gather",
+    )(cot, normed)
+
+
+def sums_kernel(
+    n_row, n_col, dots, gains, dots_out, gains_out,
+    dots_in, gains_in, dots_send, dots_recv, gains_send, gains_recv,
+):
+    row, col = lax.axis_index("row"), lax.axis_index("col")
+    greet(row, col, n_row, n_col)
+    copies = []
+    for k in range(1, n_col):
+        copies.append(
+            pltpu.make_async_remote_copy(
+                src_ref=dots,
+                dst_ref=dots_in.at[col],
+                send_sem=dots_send.at[k],
+                recv_sem=dots_recv.at[k],
+                device_id=(row, (col + k) % n_col),
+                device_id_type=MESH,
+            )
+        )
+    for k in range(1, n_row):
+        copies.append(
+            pltpu.make_async_remote_copy(
+                src_ref=gains,
+                dst_ref=gains_in.at[row],
+                send_sem=gains_send.at[k],
+                recv_sem=gains_recv.at[k],
+                device_id=((row + k) % n_row, col),
+                device_id_type=MESH,
+            )
+        )
+    for copy in copies:
+        copy.start()
+    dots_in[col] = dots[...]
+    gains_in[row] = gains[...]
+    for copy in copies:
+        copy.wait()
+    dots_out[...] = jnp.sum(dots_in[...], axis=0)
+    gains_out[...] = jnp.sum(gains_in[...], axis=0)
+
+
+def sums(dots, gains, n_row, n_col):
+    dma = pltpu.SemaphoreType.DMA
+    return pl.pallas_call(
+        functools.partial(sums_kernel, n_row, n_col),
+        out_shape=(
+            jax.ShapeDtypeStruct(dots.shape, dots.dtype),
+            jax.ShapeDtypeStruct(gains.shape, gains.dtype),
+        ),
+        in_specs=[pl.BlockSpec(memory_space=pltpu.VMEM)] * 2,
+        out_specs=[pl.BlockSpec(memory_space=pltpu.VMEM)] * 2,
+        scratch_shapes=[
+            pltpu.VMEM((n_col,) + dots.shape, dots.dtype),
+            pltpu.VMEM((n_row,) + gains.shape, gains.dtype),
+            dma((n_col,)),
+            dma((n_col,)),
+            dma((n_row,)),
+            dma((n_row,)),
+        ],
+        compiler_params=pltpu.CompilerParams(collective_id=1, has_side_effects=True),
+        name="sums",
+    )(dots, gains)
 
 
 def local(layer_input, gain, d_query, d_keyval, w_query, w_keyval, d_resid):
@@ -20,7 +225,10 @@
     contract_cols = (((1,), (1,)), ((), ()))
     query_cols = d_query.shape[1]
     cotangent = jnp.concatenate([d_query, d_keyval], axis=1)
-    all_cotangents = lax.all_gather(cotangent, "row", axis=0, tiled=True)
+    n_row, n_col = lax.axis_size("row"), lax.axis_size("col")
+    all_cotangents, columns = gather(cotangent, normed, n_row, n_col)
+    all_cotangents = all_cotangents.reshape(-1, cotangent.shape[1])
+    columns = columns.reshape(all_cotangents.shape[0], -1)
     weights = jnp.concatenate([w_query, w_keyval], axis=1)
     partial_value = lax.dot_general(
         all_cotangents, weights, contract_cols, preferred_element_type=jnp.float32
@@ -28,7 +236,6 @@
     reduced = lax.psum_scatter(
         partial_value.astype(jnp.bfloat16), "col", scatter_dimension=0, tiled=True
     )
-    n_row, n_col = lax.axis_size("row"), lax.axis_size("col")
     fold = n_row // n_col
     pieces = reduced.reshape(fold, local_tokens, reduced.shape[1])
     row, col = lax.axis_index("row"), lax.axis_index("col")
@@ -54,34 +261,31 @@
     input_part = lax.dynamic_slice_in_dim(inputs, col_start, slice_width, 1)
     gain_part = lax.dynamic_slice_in_dim(gain, col_start, slice_width, 0)
     weighted = gain_part * feature_grad
-    token_dot = lax.psum(jnp.sum(weighted * input_part, axis=1, keepdims=True), "col")
+    gain_partial = jnp.sum(feature_grad * input_part * inv_rms, axis=0) * scaling
+    dots, gains = sums(
+        jnp.sum(weighted * input_part, axis=1).reshape(-1, 128),
+        gain_partial.reshape(-1, 128),
+        n_row,
+        n_col,
+    )
+    token_dot = dots.reshape(local_tokens, 1)
+    grad_gain = gains.reshape(slice_width)
     d_input = (
         d_resid.astype(jnp.float32)
         + inv_rms * weighted
         - input_part * inv_rms**3 * token_dot / model_width
     ).astype(jnp.bfloat16)
-    gain_partial = jnp.sum(feature_grad * input_part * inv_rms, axis=0) * scaling
-    cotangent = jnp.concatenate([d_query, d_keyval], axis=1)
-    columns = lax.all_to_all(normed, "row", split_axis=1, concat_axis=0, tiled=True)
-    groups = lax.axis_size("row")
-    column_blocks = columns.reshape(groups, local_tokens, columns.shape[1])
-    grad_blocks = all_cotangents.reshape(groups, local_tokens, all_cotangents.shape[1])
-    blocks = (
+    summed = (
         lax.dot_general(
-            column_blocks,
-            grad_blocks,
-            (((1,), (1,)), ((0,), (0,))),
-            preferred_element_type=jnp.float32,
+            columns, all_cotangents, (((0,), (0,)), ((), ())), preferred_element_type=jnp.float32
         )
         * weight_scale
     )
-    summed = jnp.sum(blocks.astype(jnp.bfloat16).astype(jnp.float32), axis=0)
     grad_wq = summed[:, :query_cols].astype(jnp.bfloat16)
     grad_wkv = summed[:, query_cols:].astype(jnp.bfloat16)
     query_f = grad_wq.astype(jnp.float32)
     keyval_f = grad_wkv.astype(jnp.float32)
     tile_square = jnp.sum(query_f * query_f) + jnp.sum(keyval_f * keyval_f)
-    grad_gain = lax.psum(gain_partial, "row")
     leading = jnp.where(
         lax.axis_index("row") == 0, jnp.sum(grad_gain * grad_gain), jnp.float32(0.0)
     )

time: 377 us -> 292 us (0.77)
  waiting for transfers between devices: 198 us -> 45.3 us
  Pallas kernels: 0 us -> 129 us
  blocking collectives: 91.9 us -> 41.6 us
  starting transfers between devices: 10.2 us -> 3.87 us
  local copies, waits for them, and re-layouts: 8.93 us -> 2.92 us
    all_gather x1 -> x0, waiting for transfers between devices: 150 us -> none  [local(): all_cotangents = lax.all_gather(cotangent, 'row', axis=0, tiled=True)]
    pallas_call x0 -> x2, Pallas kernels: none -> 129 us  [the longest x1 95.3 us: gather(): pl.pallas_call(functools.partial(gather_kernel, n_row, n_col), out_shape=...]
    psum x2 -> x0, blocking collectives: 45.4 us -> none  [the longest x1 39.8 us: local(): grad_gain = lax.psum(gain_partial, 'row')]
    convert_element_type x1 -> x0, local copies, waits for them, and re-layouts: 6.45 us -> none  [local(): normed = (inputs * inv_rms * gain).astype(jnp.bfloat16)]
    all_to_all x1 -> x0, starting transfers between devices: 6.34 us -> none  [local(): lax.all_to_all(normed, 'row', split_axis=1, concat_axis=0, tiled=True)]
    psum x1, blocking collectives: 46.5 us -> 41.6 us  [local(): grand_total = lax.psum(tile_square + leading, ('row', 'col'))]
  transfers between devices with their start and end apart: 5 -> 3, of which waited for: 4 -> 3; matrix products, arithmetic and copies ran while one was open for 12% -> 7% of each run, Pallas kernels for 0% -> 0%
where the time goes in v2:
time: 292 us; the launch traced here: 291 us
  Pallas kernels  129 us (44%)
  waiting for transfers between devices  45.3 us (16%)
  blocking collectives  41.6 us (14%)
  other arithmetic  28.4 us (10%)
  matrix products  21.4 us (7%)
  between operations  18 us (6%)
  starting transfers between devices  3.87 us (1%)
  local copies, waits for them, and re-layouts  2.92 us (1%)
    pallas_call x1, Pallas kernels, gather(): pl.pallas_call(functools.partial(gather_kernel, n_row, n_col), out_shape=...  95.3 us
    psum x1, blocking collectives, local(): grand_total = lax.psum(tile_square + leading, ('row', 'col'))  41.6 us
    pallas_call x1, Pallas kernels, sums(): pl.pallas_call(functools.partial(sums_kernel, n_row, n_col), out_shape=(j...  33.8 us
    reduce_scatter x1, waiting for transfers between devices, local(): lax.psum_scatter(partial_value.astype(jnp.bfloat16), 'col', scatter_dimen...  33.7 us
    ppermute x2, waiting for transfers between devices, local(): arrived.append(lax.ppermute(piece, ('row', 'col'), pairs))  11.7 us
    dot_general x1, matrix products, local(): lax.dot_general(all_cotangents, weights, contract_cols, preferred_element...  11.2 us
    dot_general x1, matrix products, local(): lax.dot_general(columns, all_cotangents, (((0,), (0,)), ((), ())), prefer...  10.2 us
    convert_element_type x1, other arithmetic, local(): inputs = layer_input.astype(jnp.float32)  6.41 us
  transfers between devices with their start and end apart: 3, of which 3 were waited for; matrix products, arithmetic and copies ran while one was open for 7% of the time, Pallas kernels for 0%

profile of v2, /device:TPU:12, one launch (start us, length us, event | category | flops | bytes accessed | tf_op | source)
XLA Modules:
  0.0 290.6 jit_solution(14051607968802910266)
XLA Ops:
  7.2 0.0 copy-start.3
  7.2 0.0 copy-start.2
  7.2 0.0 copy-start.4
  7.2 0.0 reduce-scatter.2.cloned.1.call-start
  7.2 0.0 copy-start
  7.3 3.3 %multiply_reduce_fusion = f32[256]{0:T(256)S(1)} fusion(bf16[256,8192]{1,0:T(8,128)(2,1)} %param.7), kind=kLoop, calls=%fused_computation.1 | loop fusion | flops 6291200 | bytes 4195328 | tf_op jit(solution)/shard_map/reduce_sum | solution.py:218
  10.5 0.0 copy-done.3
  10.5 0.0 copy-done.2
  10.5 0.9 pad_maximum_fusion.1.cot
  11.5 0.0 copy-done.4
  11.5 0.0 copy-done
  11.5 3.1 %multiply_convert_fusion.normed = bf16[256,8192]{1,0:T(8,128)(2,1)} fusion(f32[8192]{0:T(1024)S(1)} %copy-done.4, f32[256]{0:T(256)S(1)} %get-tuple-element.24, bf16[256,8192]{1,0:T(8,128)(2,1)S(1)} %copy-done), kind=kLoop, calls=%fused_computation | loop fusion | flops 8388608 | bytes 8422400 | tf_op jit(solution)/shard_map/convert_element_type | solution.py:219
  14.6 0.0 copy-start.6
  14.6 0.0 copy-start.7
  14.6 95.3 %gather.1 = (bf16[8,256,1536]{2,1,0:T(8,128)(2,1)}, bf16[8,256,1024]{2,1,0:T(8,128)(2,1)}) custom-call(bf16[256,1536]{1,0:T(8,128)(2,1)} %pad_maximum_fusion.1.cot, bf16[256,8192]{1,0:T(8,128)(2,1)} %multiply_convert_fusion.normed), custom_call_target="tpu_custom_call" | custom-call | tf_op jit(solution)/shard_map/gather/pallas_call | solution.py:132
  109.9 0.0 copy-done.6
  109.9 0.0 copy-done.7
  109.9 11.2 %convolution_convert_fusion = bf16[2048,1024]{1,0:T(8,128)(2,1)} fusion(bf16[2048,1536]{1,0:T(8,128)(2,1)} %bitcast.28, bf16[1024,512]{1,0:T(8,128)(2,1)S(1)} %copy-done.7, bf16[1024,1024]{1,0:T(8,128)(2,1)S(1)} %copy-done.6), kind=kOutput, calls=%fused_computation.5 | convolution fusion | flops 6450839552 | bytes 13631488 | tf_op jit(solution)/shard_map/dot_general | solution.py:233
  121.1 0.0 reduce-scatter.2.cloned.1.call-update
  121.2 6.4 %convert_element_type.27 = f32[256,8192]{1,0:T(8,128)} convert(bf16[256,8192]{1,0:T(8,128)(2,1)} %param.7) | non-fusion elementwise | flops 2097152 | bytes 12582912 | tf_op jit(solution)/shard_map/convert_element_type | solution.py:217
  127.6 10.2 %fusion = bf16[1024,1536]{1,0:T(8,128)(2,1)S(1)} fusion(bf16[8,256,1024]{2,1,0:T(8,128)(2,1)} %get-tuple-element.11, bf16[8,256,1536]{2,1,0:T(8,128)(2,1)} %get-tuple-element.9), kind=kOutput, calls=%fused_computation.3 | convolution fusion | flops 6445596672 | bytes 13631488 | tf_op jit(solution)/shard_map/dot_general | solution.py:279
  137.8 33.7 %reduce-scatter.2.cloned.1.call-done = bf16[512,1024]{1,0:T(8,128)(2,1)} async-done(((bf16[2048,1024]{1,0:T(8,128)(2,1)}), bf16[512,1024]{1,0:T(8,128)(2,1)}) %reduce-scatter.2.cloned.1.call-update) | async-done | bytes 1048592 | tf_op jit(solution)/shard_map/reduce_scatter | solution.py:236
  171.5 2.3 dynamic-slice_bitcast_fusion
  173.8 0.0 collective-permute-start.1
  173.8 3.8 %collective-permute-start = (bf16[256,1024]{1,0:T(8,128)(2,1)}, bf16[256,1024]{1,0:T(8,128)(2,1)}, u32[]{:S(2)}, u32[]{:S(2)}) collective-permute-start(bf16[256,1024]{1,0:T(8,128)(2,1)} %get-tuple-element.22), channel_id=1, source_target_pairs={{0,0},{1,8},{2,16},{3,24},{4,4},{5,12},{6,20},{7,28},{8,1},{9,9},{... | collective-permute-start | bytes 1572872 | tf_op jit(solution)/shard_map/ppermute | solution.py:250
  177.6 2.0 multiply_reduce_fusion.2
  179.6 2.9 %multiply_reduce_fusion.1 = (f32[]{:T(128)}, bf16[1024,1024]{1,0:T(8,128)(2,1)}) fusion(bf16[1024,1536]{1,0:T(8,128)(2,1)S(1)} %fusion), kind=kLoop, calls=%fused_computation.4 | loop fusion | flops 3145727 | bytes 4194308 | tf_op jit(solution)/shard_map/reduce_sum | solution.py:288
  182.6 0.0 copy-start.1
  184.0 0.4 collective-permute-done.1
  184.4 11.2 %collective-permute-done = bf16[256,1024]{1,0:T(8,128)(2,1)} collective-permute-done((bf16[256,1024]{1,0:T(8,128)(2,1)}, bf16[256,1024]{1,0:T(8,128)(2,1)}, u32[]{:S(2)}, u32[]{:S(2)}) %collective-permute-start) | collective-permute-done | bytes 524320 | tf_op jit(solution)/shard_map/ppermute | solution.py:250
  195.6 1.6 fusion.15
  197.2 2.8 fusion.11
  200.0 0.6 multiply_bitcast_fusion.gains
  200.6 33.8 %sums.1 = (f32[2,128]{1,0:T(2,128)}, f32[16,128]{1,0:T(8,128)}) custom-call(f32[2,128]{1,0:T(2,128)} %bitcast.26, f32[16,128]{1,0:T(8,128)} %multiply_bitcast_fusion.gains), custom_call_target="tpu_custom_call" | custom-call | tf_op jit(solution)/shard_map/sums/pallas_call | solution.py:195
  234.4 0.0 copy-start.5
  234.4 1.4 multiply_reduce_fusion.3
  236.4 41.6 %psum.7 = f32[]{:T(128)} all-reduce(f32[]{:T(128)S(6)} %add.76), channel_id=1, replica_groups=mesh['row'=8,'col'=4] {'row','col'}, use_global_device_ids=true, to_apply=%region_7.8 | all-reduce | flops 1 | bytes 8 | tf_op jit(solution)/shard_map/psum | solution.py:292
  278.7 0.0 copy-done.1
  278.7 3.3 %fusion.8 = bf16[256,2048]{1,0:T(8,128)(2,1)} fusion(bf16[256,2048]{1,0:T(8,128)(2,1)S(1)} %copy-done.1, f32[256,8192]{1,0:T(8,128)} %convert_element_type.27, s32[]{:T(128)S(6)} %select_n.36, f32[256]{0:T(256)} %bitcast.27, f32[256]{0:T(256)S(1)} %get-tuple-element.23, f32[2048]{0:T(1024)S(1)} %dynamic_slice.19, f32[256]{0:T(256)S(1)} %get-tuple-element.24, ...), kind=kLoop, calls=%fused_computation.15 | loop fusion | flops 6815744 | bytes 5254148 | tf_op jit(solution)/shard_map/convert_element_type | solution.py:277
  282.1 0.0 copy-done.5
  282.1 0.6 copy.15
  (2 shorter events, 0.0 us)
Async XLA Ops:
  7.2 3.4 %copy-start.3 = (bf16[256,512]{1,0:T(8,128)(2,1)S(1)}, bf16[256,512]{1,0:T(8,128)(2,1)}, u32[]{:S(2)}) copy-start(bf16[256,512]{1,0:T(8,128)(2,1)} %param.10) | copy-start | bytes 786436
  7.2 3.4 %copy-start.2 = (bf16[256,1024]{1,0:T(8,128)(2,1)S(1)}, bf16[256,1024]{1,0:T(8,128)(2,1)}, u32[]{:S(2)}) copy-start(bf16[256,1024]{1,0:T(8,128)(2,1)} %param.9) | copy-start | bytes 1572868
  7.2 4.3 %copy-start.4 = (f32[8192]{0:T(1024)S(1)}, f32[8192]{0:T(1024)}, u32[]{:S(2)}) copy-start(f32[8192]{0:T(1024)} %param.8) | copy-start | bytes 98308
  7.2 164.3 %reduce-scatter.2.cloned.1.call-start = ((), (), s32[]{:S(2)}) async-start(), calls=%async_computation.1 | async-start | bytes 5242880 | tf_op jit(solution)/shard_map/reduce_scatter | solution.py:236
  7.2 4.2 %copy-start = (bf16[256,8192]{1,0:T(8,128)(2,1)S(1)}, bf16[256,8192]{1,0:T(8,128)(2,1)}, u32[]{:S(2)}) copy-start(bf16[256,8192]{1,0:T(8,128)(2,1)} %param.7) | copy-start | bytes 12582916
  14.6 95.3 %copy-start.6 = (bf16[1024,1024]{1,0:T(8,128)(2,1)S(1)}, bf16[1024,1024]{1,0:T(8,128)(2,1)}, u32[]{:S(2)}) copy-start(bf16[1024,1024]{1,0:T(8,128)(2,1)} %param.11) | copy-start | bytes 6291460
  14.6 95.3 %copy-start.7 = (bf16[1024,512]{1,0:T(8,128)(2,1)S(1)}, bf16[1024,512]{1,0:T(8,128)(2,1)}, u32[]{:S(2)}) copy-start(bf16[1024,512]{1,0:T(8,128)(2,1)} %param.12) | copy-start | bytes 3145732
  173.8 10.6 %collective-permute-start.1 = (bf16[256,1024]{1,0:T(8,128)(2,1)}, bf16[256,1024]{1,0:T(8,128)(2,1)}, u32[]{:S(2)}, u32[]{:S(2)}) collective-permute-start(bf16[256,1024]{1,0:T(8,128)(2,1)} %get-tuple-element.21), channel_id=1, source_target_pairs={{0,4},{1,12},{2,20},{3,28},{4,0},{5,8},{6,16},{7,24},{8,5},{9,13},... | collective-permute-start | bytes 1572872 | tf_op jit(solution)/shard_map/ppermute | solution.py:250
  173.8 21.9 %collective-permute-start = (bf16[256,1024]{1,0:T(8,128)(2,1)}, bf16[256,1024]{1,0:T(8,128)(2,1)}, u32[]{:S(2)}, u32[]{:S(2)}) collective-permute-start(bf16[256,1024]{1,0:T(8,128)(2,1)} %get-tuple-element.22), channel_id=1, source_target_pairs={{0,0},{1,8},{2,16},{3,24},{4,4},{5,12},{6,20},{7,28},{8,1},{9,9},{... | collective-permute-start | bytes 1572872 | tf_op jit(solution)/shard_map/ppermute | solution.py:250
  182.6 96.1 %copy-start.1 = (bf16[256,2048]{1,0:T(8,128)(2,1)S(1)}, bf16[256,2048]{1,0:T(8,128)(2,1)}, u32[]{:S(2)}) copy-start(bf16[256,2048]{1,0:T(8,128)(2,1)} %param.13) | copy-start | bytes 3145732
  234.4 47.6 %copy-start.5 = (f32[16,128]{1,0:T(8,128)S(1)}, f32[16,128]{1,0:T(8,128)}, u32[]{:S(2)}) copy-start(f32[16,128]{1,0:T(8,128)} %get-tuple-element.12) | copy-start | bytes 24580
Sparse Core Ops, SparseCore 0:
  121.2 50.1 reduce-scatter.1
